TPU v7x, 32 devices: a whole 2x2x4 slice. The times are simulated.
32 devices in a mesh: section: 4 (over y, x), mp: 8 (over z, core).
Axes of the slice: x: 2, y: 2, z: 4, core: 2. Of those that a mesh axis runs over, the one named last changes fastest.
Arguments:
- hidden_in: bfloat16 [1, 4, 64, 4096], P(None, 'section'), may hold values from -36 to 36
- attn_gain: bfloat16 [4, 4096], P('section'), may hold values from 0.5 to 2
- w_query: bfloat16 [4, 4096, 4096], P('section', None, 'mp'), may hold values from -0.75 to 0.75
- w_key: bfloat16 [4, 4096, 1024], P('section', None, 'mp'), may hold values from -0.0625 to 0.0625
- w_value: bfloat16 [4, 4096, 1024], P('section', None, 'mp'), may hold values from -0.09375 to 0.09375
- w_out: bfloat16 [4, 4096, 4096], P('section', 'mp'), may hold values from -0.09375 to 0.09375
- ffn_gain: bfloat16 [4, 4096], P('section'), may hold values from 0.5 to 2
- w_gate: bfloat16 [4, 4096, 14336], P('section', None, 'mp'), may hold values from -0.09375 to 0.09375
- w_up: bfloat16 [4, 4096, 14336], P('section', None, 'mp'), may hold values from -0.09375 to 0.09375
- w_down: bfloat16 [4, 14336, 4096], P('section', 'mp'), may hold values from -0.046875 to 0.046875
- ffn_blocks: int32 [4, 4], P(None, 'section'), may hold values from 1 to 112
- heads_on: int32 [4, 4], P(None, 'section'), may hold values from 1 to 32
Outputs:
- hidden_out: bfloat16 [1, 4, 64, 4096], P(None, 'section')
Inputs may be any that keep to these rules, and one draw needn't show every extreme that they name: `ffn_blocks`: hidden units below 128 times the entry are active. `heads_on`: query heads below the entry are active.
All inputs are finite; a program needn't handle non-finite values.
Results may differ from a plain program's by a relative error of at most 0.025.
Values may be sent and summed in bfloat16 or wider, within the bound.
A program may use at most 128 MiB of HBM per device.

v0:
```python
import jax
import jax.numpy as jnp
from jax import lax
from jax.sharding import PartitionSpec as P

HEADS = 32
KV_HEADS = 8
HD = 128
BLOCK = 128


ROPE_BASE = 500000.0
EPSILON = 1e-05


def passed_along(array, axis, by):
    peers = lax.axis_size(axis)
    return lax.ppermute(array, axis, [(i, (i + by) % peers) for i in range(peers)])


def rms_scale(values, gain_row):
    mean_sq = jnp.mean(values * values, axis=-1, keepdims=True)
    return values * lax.rsqrt(mean_sq + EPSILON) * gain_row.astype(jnp.float32)


def rotate(values):
    length = values.shape[0]
    half_dim = values.shape[-1] // 2
    frequency = ROPE_BASE ** (-(jnp.arange(half_dim, dtype=jnp.float32) / half_dim))
    angles = jnp.arange(length, dtype=jnp.float32)[:, None] * frequency[None, :]
    cosine_table = jnp.cos(angles)[:, None, :]
    sine_table = jnp.sin(angles)[:, None, :]
    front_half = values[..., :half_dim].astype(jnp.float32)
    back_half = values[..., half_dim:].astype(jnp.float32)
    return jnp.concatenate(
        [
            front_half * cosine_table - back_half * sine_table,
            front_half * sine_table + back_half * cosine_table,
        ],
        axis=-1,
    )


def attend_local(projected, query_width, key_width, active, first_head):
    length = projected.shape[0]
    heads_here = query_width // HD
    group_size = HEADS // KV_HEADS
    queries = rotate(projected[:, :query_width].reshape(length, heads_here, HD)).astype(
        jnp.bfloat16
    )
    key_local = projected[:, query_width : query_width + key_width].astype(jnp.bfloat16)
    value_local = projected[:, query_width + key_width :].astype(jnp.bfloat16)
    key_whole, value_whole = (
        lax.all_gather(key_local, "mp", axis=1, tiled=True),
        lax.all_gather(value_local, "mp", axis=1, tiled=True),
    )
    key_heads = key_whole.reshape(length, HD, KV_HEADS).transpose(0, 2, 1)
    value_heads = value_whole.reshape(length, HD, KV_HEADS).transpose(0, 2, 1)
    kv_here = max(1, heads_here // group_size)
    repeat_count = heads_here // kv_here
    first_kv = first_head // group_size
    key_pick = lax.dynamic_slice_in_dim(key_heads, first_kv, kv_here, 1)
    value_pick = lax.dynamic_slice_in_dim(value_heads, first_kv, kv_here, 1)
    keys_rot = jnp.repeat(rotate(key_pick).astype(jnp.bfloat16), repeat_count, axis=1)
    values = jnp.repeat(value_pick, repeat_count, axis=1)
    scores = jnp.einsum(
        "qhd,khd->hqk", queries, keys_rot, preferred_element_type=jnp.float32
    ) * HD ** (-0.5)
    causal = jnp.arange(length)[:, None] >= jnp.arange(length)[None, :]
    scores = jnp.where(causal[None], scores, -jnp.inf)
    probabilities = jax.nn.softmax(scores, axis=-1).astype(jnp.bfloat16)
    context = jnp.einsum("hqk,khd->qhd", probabilities, values, preferred_element_type=jnp.float32)
    head_ids = first_head + jnp.arange(heads_here)
    context = jnp.where((head_ids < active)[None, :, None], context, 0.0).astype(jnp.bfloat16)
    return context.reshape(length, query_width)


def per_device(
    hidden_in,
    attn_gain,
    w_query,
    w_key,
    w_value,
    w_out,
    ffn_gain,
    w_gate,
    w_up,
    w_down,
    ffn_blocks,
    heads_on,
):
    section_count = lax.axis_size("section")
    section_index = lax.axis_index("section")
    model_count = lax.axis_size("mp")
    model_index = lax.axis_index("mp")
    micro_total = ffn_blocks.shape[0]
    per_section = hidden_in.shape[0]
    length = hidden_in.shape[2]
    model_width = hidden_in.shape[3]
    local_rows = length // model_count
    units_here = w_gate.shape[2]
    query_width = w_query.shape[2]
    key_width = w_key.shape[2]
    first_head = model_index * (query_width // HD)
    first_unit = model_index * units_here
    joined_qkv = [jnp.concatenate([w_query[0], w_key[0], w_value[0]], axis=1)]
    joined_pair = [jnp.concatenate([w_gate[0], w_up[0]], axis=1)]

    def gated(pre_act, block_count):
        gate_part = pre_act[:, :units_here]
        up_part = pre_act[:, units_here:]
        unit_ids = first_unit + jnp.arange(units_here)
        return jnp.where(
            (unit_ids < BLOCK * block_count)[None, :], jax.nn.silu(gate_part) * up_part, 0.0
        ).astype(jnp.bfloat16)

    def layer_rows(carried, layer_pos, active, block_count):
        residual = carried.astype(jnp.float32)
        normed = rms_scale(residual, attn_gain[layer_pos]).astype(jnp.bfloat16)
        projected = jnp.dot(
            lax.all_gather(normed, "mp", axis=0, tiled=True),
            joined_qkv[layer_pos],
            preferred_element_type=jnp.float32,
        )
        context = attend_local(projected, query_width, key_width, active, first_head)
        attended = residual + lax.psum_scatter(
            jnp.dot(context, w_out[layer_pos], preferred_element_type=jnp.float32).astype(
                jnp.bfloat16
            ),
            "mp",
            scatter_dimension=0,
            tiled=True,
        ).astype(jnp.float32)
        normed_ffn = rms_scale(attended, ffn_gain[layer_pos]).astype(jnp.bfloat16)
        hidden = gated(
            jnp.dot(
                lax.all_gather(normed_ffn, "mp", axis=0, tiled=True),
                joined_pair[layer_pos],
                preferred_element_type=jnp.float32,
            ),
            block_count,
        )
        return (
            attended
            + lax.psum_scatter(
                jnp.dot(hidden, w_down[layer_pos], preferred_element_type=jnp.float32).astype(
                    jnp.bfloat16
                ),
                "mp",
                scatter_dimension=0,
                tiled=True,
            ).astype(jnp.float32)
        ).astype(jnp.bfloat16)

    def section_work(carried, moment, layer_fn):
        micro_index = jnp.clip(moment - section_index, 0, micro_total - 1)
        carried = layer_fn(carried, 0, heads_on[micro_index, 0], ffn_blocks[micro_index, 0])
        return carried

    def tick_step(moment, loop_carry):
        carried, slot_buffer = loop_carry
        cycle_index = moment // section_count
        incoming = lax.dynamic_index_in_dim(
            slot_buffer, jnp.minimum(cycle_index, per_section - 1), 0, keepdims=False
        )
        incoming = jnp.where(moment < micro_total, incoming, jnp.zeros_like(incoming))
        at_head = section_index == 0
        written = lax.dynamic_update_index_in_dim(
            slot_buffer, carried, jnp.maximum(cycle_index - 1, 0), 0
        )
        slot_buffer = jnp.where(at_head & (moment >= section_count), written, slot_buffer)
        carried = jnp.where(at_head, incoming, carried)
        carried = section_work(carried, moment, layer_rows)
        carried = passed_along(carried, "section", 1)
        slot_buffer = passed_along(slot_buffer, "section", -1)
        return (carried, slot_buffer)

    slot_start = hidden_in.reshape(per_section, length, model_width)
    slot_start = lax.dynamic_slice_in_dim(slot_start, model_index * local_rows, local_rows, 1)
    initial = jnp.zeros((local_rows, model_width), jnp.bfloat16)
    finished = lax.fori_loop(0, micro_total + section_count, tick_step, (initial, slot_start))
    result = finished[1]
    result = lax.all_gather(result, "mp", axis=1, tiled=True)
    return result.reshape(hidden_in.shape)


def solution(mesh):
    return jax.shard_map(
        per_device,
        mesh=mesh,
        in_specs=(
            P(None, "section", None, None),
            P("section", None),
            P("section", None, "mp"),
            P("section", None, "mp"),
            P("section", None, "mp"),
            P("section", "mp", None),
            P("section", None),
            P("section", None, "mp"),
            P("section", None, "mp"),
            P("section", "mp", None),
            P(None, "section"),
            P(None, "section"),
        ),
        out_specs=P(None, "section", None, None),
        check_vma=False,
    )
```

profile of v0, /device:TPU:7, one launch (start us, length us, event | category | flops | bytes accessed | tf_op | source)
XLA Modules:
  0.0 1253.7 jit_solution(6768073493346036142)
XLA Ops:
  14.0 20.1 %pad_maximum_fusion.1 = bf16[4096,3584]{1,0:T(8,128)(2,1)} fusion(bf16[4096,1792]{1,0:T(8,128)(2,1)} %bitcast.81, bf16[4096,1792]{1,0:T(8,128)(2,1)} %bitcast.82), kind=kLoop, calls=%fused_computation.74 | loop fusion | flops 58720256 | bytes 58720256 | tf_op jit(solution)/shard_map/concatenate | solution.py:107
  34.2 1192.6 %while.18 = (s32[]{:T(128)}, bf16[8,4096]{1,0:T(8,128)(2,1)S(1)}, bf16[1,8,4096]{2,1,0:T(8,128)(2,1)S(1)}, pred[]{:T(512)}, s32[]{:T(128)}, /*index=5*/s32[]{:T(...) while((s32[]{:T(128)}, bf16[8,4096]{1,0:T(8,128)(2,1)S(1)}, ...), condition=%wide.region_7.8_spmd, body=%wide.region_0.7_spmd.sunk | while | flops 3500834560 | bytes 112000056 | solution.py:181
  34.7 15.5 %all_gather.48 = bf16[64,4096]{1,0:T(8,128)(2,1)S(1)} all-gather(bf16[8,4096]{1,0:T(8,128)(2,1)S(1)} %fusion.103), channel_id=1, replica_groups=mesh['section'=4,'mp'=8] {'mp'}, dimensions={0}, use_global_device_ids=true | all-gather | bytes 589824 | tf_op jit(solution)/shard_map/while/body/eval_jaxpr/all_gather | solution.py:121
  54.3 12.8 %all_gather.49 = bf16[64,1024]{1,0:T(8,128)(2,1)S(1)} all-gather(bf16[64,128]{1,0:T(8,128)(2,1)S(1)} %get-tuple-element.607), channel_id=1, replica_groups=mesh['section'=4,'mp'=8] {'mp'}, dimensions={1}, use_global_device_ids=true | all-gather | bytes 147456 | tf_op jit(solution)/shard_map/while/body/eval_jaxpr/all_gather | solution.py:54
  67.3 12.8 %all_gather.50 = bf16[64,1024]{1,0:T(8,128)(2,1)S(1)} all-gather(bf16[64,128]{1,0:T(8,128)(2,1)S(1)} %get-tuple-element.608), channel_id=1, replica_groups=mesh['section'=4,'mp'=8] {'mp'}, dimensions={1}, use_global_device_ids=true | all-gather | bytes 147456 | tf_op jit(solution)/shard_map/while/body/eval_jaxpr/all_gather | solution.py:55
  88.2 25.2 %reduce-scatter.3.cloned.1.call-done = bf16[8,4096]{1,0:T(8,128)(2,1)} async-done(((bf16[64,4096]{1,0:T(8,128)(2,1)}), bf16[8,4096]{1,0:T(8,128)(2,1)}) %reduce-scatter.3.cloned.1.call-update) | async-done | bytes 65552 | tf_op jit(solution)/shard_map/while/body/eval_jaxpr/reduce_scatter | solution.py:126
  115.3 18.5 %all_gather.51 = bf16[64,4096]{1,0:T(8,128)(2,1)S(1)} all-gather(bf16[8,4096]{1,0:T(8,128)(2,1)S(1)} %multiply_convert_fusion.2), channel_id=1, replica_groups=mesh['section'=4,'mp'=8] {'mp'}, dimensions={0}, use_global_device_ids=true | all-gather | bytes 589824 | tf_op jit(solution)/shard_map/while/body/eval_jaxpr/all_gather | solution.py:137
  150.0 25.8 %reduce-scatter.5.cloned.1.call-done = bf16[8,4096]{1,0:T(8,128)(2,1)} async-done(((bf16[64,4096]{1,0:T(8,128)(2,1)}), bf16[8,4096]{1,0:T(8,128)(2,1)}) %reduce-scatter.5.cloned.1.call-update) | async-done | bytes 65552 | tf_op jit(solution)/shard_map/while/body/eval_jaxpr/reduce_scatter | solution.py:145
  180.3 19.9 %all_gather.48 = bf16[64,4096]{1,0:T(8,128)(2,1)S(1)} all-gather(bf16[8,4096]{1,0:T(8,128)(2,1)S(1)} %fusion.103), channel_id=1, replica_groups=mesh['section'=4,'mp'=8] {'mp'}, dimensions={0}, use_global_device_ids=true | all-gather | bytes 589824 | tf_op jit(solution)/shard_map/while/body/eval_jaxpr/all_gather | solution.py:121
  204.3 12.8 %all_gather.49 = bf16[64,1024]{1,0:T(8,128)(2,1)S(1)} all-gather(bf16[64,128]{1,0:T(8,128)(2,1)S(1)} %get-tuple-element.607), channel_id=1, replica_groups=mesh['section'=4,'mp'=8] {'mp'}, dimensions={1}, use_global_device_ids=true | all-gather | bytes 147456 | tf_op jit(solution)/shard_map/while/body/eval_jaxpr/all_gather | solution.py:54
  217.3 12.8 %all_gather.50 = bf16[64,1024]{1,0:T(8,128)(2,1)S(1)} all-gather(bf16[64,128]{1,0:T(8,128)(2,1)S(1)} %get-tuple-element.608), channel_id=1, replica_groups=mesh['section'=4,'mp'=8] {'mp'}, dimensions={1}, use_global_device_ids=true | all-gather | bytes 147456 | tf_op jit(solution)/shard_map/while/body/eval_jaxpr/all_gather | solution.py:55
  238.2 24.9 %reduce-scatter.3.cloned.1.call-done = bf16[8,4096]{1,0:T(8,128)(2,1)} async-done(((bf16[64,4096]{1,0:T(8,128)(2,1)}), bf16[8,4096]{1,0:T(8,128)(2,1)}) %reduce-scatter.3.cloned.1.call-update) | async-done | bytes 65552 | tf_op jit(solution)/shard_map/while/body/eval_jaxpr/reduce_scatter | solution.py:126
  265.0 18.6 %all_gather.51 = bf16[64,4096]{1,0:T(8,128)(2,1)S(1)} all-gather(bf16[8,4096]{1,0:T(8,128)(2,1)S(1)} %multiply_convert_fusion.2), channel_id=1, replica_groups=mesh['section'=4,'mp'=8] {'mp'}, dimensions={0}, use_global_device_ids=true | all-gather | bytes 589824 | tf_op jit(solution)/shard_map/while/body/eval_jaxpr/all_gather | solution.py:137
  299.9 25.7 %reduce-scatter.5.cloned.1.call-done = bf16[8,4096]{1,0:T(8,128)(2,1)} async-done(((bf16[64,4096]{1,0:T(8,128)(2,1)}), bf16[8,4096]{1,0:T(8,128)(2,1)}) %reduce-scatter.5.cloned.1.call-update) | async-done | bytes 65552 | tf_op jit(solution)/shard_map/while/body/eval_jaxpr/reduce_scatter | solution.py:145
  330.1 19.5 %all_gather.48 = bf16[64,4096]{1,0:T(8,128)(2,1)S(1)} all-gather(bf16[8,4096]{1,0:T(8,128)(2,1)S(1)} %fusion.103), channel_id=1, replica_groups=mesh['section'=4,'mp'=8] {'mp'}, dimensions={0}, use_global_device_ids=true | all-gather | bytes 589824 | tf_op jit(solution)/shard_map/while/body/eval_jaxpr/all_gather | solution.py:121
  353.6 12.8 %all_gather.49 = bf16[64,1024]{1,0:T(8,128)(2,1)S(1)} all-gather(bf16[64,128]{1,0:T(8,128)(2,1)S(1)} %get-tuple-element.607), channel_id=1, replica_groups=mesh['section'=4,'mp'=8] {'mp'}, dimensions={1}, use_global_device_ids=true | all-gather | bytes 147456 | tf_op jit(solution)/shard_map/while/body/eval_jaxpr/all_gather | solution.py:54
  366.7 12.8 %all_gather.50 = bf16[64,1024]{1,0:T(8,128)(2,1)S(1)} all-gather(bf16[64,128]{1,0:T(8,128)(2,1)S(1)} %get-tuple-element.608), channel_id=1, replica_groups=mesh['section'=4,'mp'=8] {'mp'}, dimensions={1}, use_global_device_ids=true | all-gather | bytes 147456 | tf_op jit(solution)/shard_map/while/body/eval_jaxpr/all_gather | solution.py:55
  387.5 25.1 %reduce-scatter.3.cloned.1.call-done = bf16[8,4096]{1,0:T(8,128)(2,1)} async-done(((bf16[64,4096]{1,0:T(8,128)(2,1)}), bf16[8,4096]{1,0:T(8,128)(2,1)}) %reduce-scatter.3.cloned.1.call-update) | async-done | bytes 65552 | tf_op jit(solution)/shard_map/while/body/eval_jaxpr/reduce_scatter | solution.py:126
  414.6 18.6 %all_gather.51 = bf16[64,4096]{1,0:T(8,128)(2,1)S(1)} all-gather(bf16[8,4096]{1,0:T(8,128)(2,1)S(1)} %multiply_convert_fusion.2), channel_id=1, replica_groups=mesh['section'=4,'mp'=8] {'mp'}, dimensions={0}, use_global_device_ids=true | all-gather | bytes 589824 | tf_op jit(solution)/shard_map/while/body/eval_jaxpr/all_gather | solution.py:137
  449.6 25.7 %reduce-scatter.5.cloned.1.call-done = bf16[8,4096]{1,0:T(8,128)(2,1)} async-done(((bf16[64,4096]{1,0:T(8,128)(2,1)}), bf16[8,4096]{1,0:T(8,128)(2,1)}) %reduce-scatter.5.cloned.1.call-update) | async-done | bytes 65552 | tf_op jit(solution)/shard_map/while/body/eval_jaxpr/reduce_scatter | solution.py:145
  479.7 19.6 %all_gather.48 = bf16[64,4096]{1,0:T(8,128)(2,1)S(1)} all-gather(bf16[8,4096]{1,0:T(8,128)(2,1)S(1)} %fusion.103), channel_id=1, replica_groups=mesh['section'=4,'mp'=8] {'mp'}, dimensions={0}, use_global_device_ids=true | all-gather | bytes 589824 | tf_op jit(solution)/shard_map/while/body/eval_jaxpr/all_gather | solution.py:121
  503.4 12.8 %all_gather.49 = bf16[64,1024]{1,0:T(8,128)(2,1)S(1)} all-gather(bf16[64,128]{1,0:T(8,128)(2,1)S(1)} %get-tuple-element.607), channel_id=1, replica_groups=mesh['section'=4,'mp'=8] {'mp'}, dimensions={1}, use_global_device_ids=true | all-gather | bytes 147456 | tf_op jit(solution)/shard_map/while/body/eval_jaxpr/all_gather | solution.py:54
  516.4 12.8 %all_gather.50 = bf16[64,1024]{1,0:T(8,128)(2,1)S(1)} all-gather(bf16[64,128]{1,0:T(8,128)(2,1)S(1)} %get-tuple-element.608), channel_id=1, replica_groups=mesh['section'=4,'mp'=8] {'mp'}, dimensions={1}, use_global_device_ids=true | all-gather | bytes 147456 | tf_op jit(solution)/shard_map/while/body/eval_jaxpr/all_gather | solution.py:55
  537.3 24.9 %reduce-scatter.3.cloned.1.call-done = bf16[8,4096]{1,0:T(8,128)(2,1)} async-done(((bf16[64,4096]{1,0:T(8,128)(2,1)}), bf16[8,4096]{1,0:T(8,128)(2,1)}) %reduce-scatter.3.cloned.1.call-update) | async-done | bytes 65552 | tf_op jit(solution)/shard_map/while/body/eval_jaxpr/reduce_scatter | solution.py:126
  564.1 18.6 %all_gather.51 = bf16[64,4096]{1,0:T(8,128)(2,1)S(1)} all-gather(bf16[8,4096]{1,0:T(8,128)(2,1)S(1)} %multiply_convert_fusion.2), channel_id=1, replica_groups=mesh['section'=4,'mp'=8] {'mp'}, dimensions={0}, use_global_device_ids=true | all-gather | bytes 589824 | tf_op jit(solution)/shard_map/while/body/eval_jaxpr/all_gather | solution.py:137
  599.0 25.8 %reduce-scatter.5.cloned.1.call-done = bf16[8,4096]{1,0:T(8,128)(2,1)} async-done(((bf16[64,4096]{1,0:T(8,128)(2,1)}), bf16[8,4096]{1,0:T(8,128)(2,1)}) %reduce-scatter.5.cloned.1.call-update) | async-done | bytes 65552 | tf_op jit(solution)/shard_map/while/body/eval_jaxpr/reduce_scatter | solution.py:145
  629.2 19.6 %all_gather.48 = bf16[64,4096]{1,0:T(8,128)(2,1)S(1)} all-gather(bf16[8,4096]{1,0:T(8,128)(2,1)S(1)} %fusion.103), channel_id=1, replica_groups=mesh['section'=4,'mp'=8] {'mp'}, dimensions={0}, use_global_device_ids=true | all-gather | bytes 589824 | tf_op jit(solution)/shard_map/while/body/eval_jaxpr/all_gather | solution.py:121
  652.9 12.8 %all_gather.49 = bf16[64,1024]{1,0:T(8,128)(2,1)S(1)} all-gather(bf16[64,128]{1,0:T(8,128)(2,1)S(1)} %get-tuple-element.607), channel_id=1, replica_groups=mesh['section'=4,'mp'=8] {'mp'}, dimensions={1}, use_global_device_ids=true | all-gather | bytes 147456 | tf_op jit(solution)/shard_map/while/body/eval_jaxpr/all_gather | solution.py:54
  665.9 12.8 %all_gather.50 = bf16[64,1024]{1,0:T(8,128)(2,1)S(1)} all-gather(bf16[64,128]{1,0:T(8,128)(2,1)S(1)} %get-tuple-element.608), channel_id=1, replica_groups=mesh['section'=4,'mp'=8] {'mp'}, dimensions={1}, use_global_device_ids=true | all-gather | bytes 147456 | tf_op jit(solution)/shard_map/while/body/eval_jaxpr/all_gather | solution.py:55
  686.7 24.9 %reduce-scatter.3.cloned.1.call-done = bf16[8,4096]{1,0:T(8,128)(2,1)} async-done(((bf16[64,4096]{1,0:T(8,128)(2,1)}), bf16[8,4096]{1,0:T(8,128)(2,1)}) %reduce-scatter.3.cloned.1.call-update) | async-done | bytes 65552 | tf_op jit(solution)/shard_map/while/body/eval_jaxpr/reduce_scatter | solution.py:126
  713.5 18.6 %all_gather.51 = bf16[64,4096]{1,0:T(8,128)(2,1)S(1)} all-gather(bf16[8,4096]{1,0:T(8,128)(2,1)S(1)} %multiply_convert_fusion.2), channel_id=1, replica_groups=mesh['section'=4,'mp'=8] {'mp'}, dimensions={0}, use_global_device_ids=true | all-gather | bytes 589824 | tf_op jit(solution)/shard_map/while/body/eval_jaxpr/all_gather | solution.py:137
  748.4 25.8 %reduce-scatter.5.cloned.1.call-done = bf16[8,4096]{1,0:T(8,128)(2,1)} async-done(((bf16[64,4096]{1,0:T(8,128)(2,1)}), bf16[8,4096]{1,0:T(8,128)(2,1)}) %reduce-scatter.5.cloned.1.call-update) | async-done | bytes 65552 | tf_op jit(solution)/shard_map/while/body/eval_jaxpr/reduce_scatter | solution.py:145
  778.7 19.6 %all_gather.48 = bf16[64,4096]{1,0:T(8,128)(2,1)S(1)} all-gather(bf16[8,4096]{1,0:T(8,128)(2,1)S(1)} %fusion.103), channel_id=1, replica_groups=mesh['section'=4,'mp'=8] {'mp'}, dimensions={0}, use_global_device_ids=true | all-gather | bytes 589824 | tf_op jit(solution)/shard_map/while/body/eval_jaxpr/all_gather | solution.py:121
  802.3 12.8 %all_gather.49 = bf16[64,1024]{1,0:T(8,128)(2,1)S(1)} all-gather(bf16[64,128]{1,0:T(8,128)(2,1)S(1)} %get-tuple-element.607), channel_id=1, replica_groups=mesh['section'=4,'mp'=8] {'mp'}, dimensions={1}, use_global_device_ids=true | all-gather | bytes 147456 | tf_op jit(solution)/shard_map/while/body/eval_jaxpr/all_gather | solution.py:54
  836.2 25.0 %reduce-scatter.3.cloned.1.call-done = bf16[8,4096]{1,0:T(8,128)(2,1)} async-done(((bf16[64,4096]{1,0:T(8,128)(2,1)}), bf16[8,4096]{1,0:T(8,128)(2,1)}) %reduce-scatter.3.cloned.1.call-update) | async-done | bytes 65552 | tf_op jit(solution)/shard_map/while/body/eval_jaxpr/reduce_scatter | solution.py:126
  863.2 18.6 %all_gather.51 = bf16[64,4096]{1,0:T(8,128)(2,1)S(1)} all-gather(bf16[8,4096]{1,0:T(8,128)(2,1)S(1)} %multiply_convert_fusion.2), channel_id=1, replica_groups=mesh['section'=4,'mp'=8] {'mp'}, dimensions={0}, use_global_device_ids=true | all-gather | bytes 589824 | tf_op jit(solution)/shard_map/while/body/eval_jaxpr/all_gather | solution.py:137
  898.1 25.6 %reduce-scatter.5.cloned.1.call-done = bf16[8,4096]{1,0:T(8,128)(2,1)} async-done(((bf16[64,4096]{1,0:T(8,128)(2,1)}), bf16[8,4096]{1,0:T(8,128)(2,1)}) %reduce-scatter.5.cloned.1.call-update) | async-done | bytes 65552 | tf_op jit(solution)/shard_map/while/body/eval_jaxpr/reduce_scatter | solution.py:145
  928.3 19.6 %all_gather.48 = bf16[64,4096]{1,0:T(8,128)(2,1)S(1)} all-gather(bf16[8,4096]{1,0:T(8,128)(2,1)S(1)} %fusion.103), channel_id=1, replica_groups=mesh['section'=4,'mp'=8] {'mp'}, dimensions={0}, use_global_device_ids=true | all-gather | bytes 589824 | tf_op jit(solution)/shard_map/while/body/eval_jaxpr/all_gather | solution.py:121
  964.9 12.8 %all_gather.50 = bf16[64,1024]{1,0:T(8,128)(2,1)S(1)} all-gather(bf16[64,128]{1,0:T(8,128)(2,1)S(1)} %get-tuple-element.608), channel_id=1, replica_groups=mesh['section'=4,'mp'=8] {'mp'}, dimensions={1}, use_global_device_ids=true | all-gather | bytes 147456 | tf_op jit(solution)/shard_map/while/body/eval_jaxpr/all_gather | solution.py:55
  985.8 25.0 %reduce-scatter.3.cloned.1.call-done = bf16[8,4096]{1,0:T(8,128)(2,1)} async-done(((bf16[64,4096]{1,0:T(8,128)(2,1)}), bf16[8,4096]{1,0:T(8,128)(2,1)}) %reduce-scatter.3.cloned.1.call-update) | async-done | bytes 65552 | tf_op jit(solution)/shard_map/while/body/eval_jaxpr/reduce_scatter | solution.py:126
  1012.7 18.6 %all_gather.51 = bf16[64,4096]{1,0:T(8,128)(2,1)S(1)} all-gather(bf16[8,4096]{1,0:T(8,128)(2,1)S(1)} %multiply_convert_fusion.2), channel_id=1, replica_groups=mesh['section'=4,'mp'=8] {'mp'}, dimensions={0}, use_global_device_ids=true | all-gather | bytes 589824 | tf_op jit(solution)/shard_map/while/body/eval_jaxpr/all_gather | solution.py:137
  1047.6 25.7 %reduce-scatter.5.cloned.1.call-done = bf16[8,4096]{1,0:T(8,128)(2,1)} async-done(((bf16[64,4096]{1,0:T(8,128)(2,1)}), bf16[8,4096]{1,0:T(8,128)(2,1)}) %reduce-scatter.5.cloned.1.call-update) | async-done | bytes 65552 | tf_op jit(solution)/shard_map/while/body/eval_jaxpr/reduce_scatter | solution.py:145
  1077.8 19.7 %all_gather.48 = bf16[64,4096]{1,0:T(8,128)(2,1)S(1)} all-gather(bf16[8,4096]{1,0:T(8,128)(2,1)S(1)} %fusion.103), channel_id=1, replica_groups=mesh['section'=4,'mp'=8] {'mp'}, dimensions={0}, use_global_device_ids=true | all-gather | bytes 589824 | tf_op jit(solution)/shard_map/while/body/eval_jaxpr/all_gather | solution.py:121
  1114.5 12.8 %all_gather.50 = bf16[64,1024]{1,0:T(8,128)(2,1)S(1)} all-gather(bf16[64,128]{1,0:T(8,128)(2,1)S(1)} %get-tuple-element.608), channel_id=1, replica_groups=mesh['section'=4,'mp'=8] {'mp'}, dimensions={1}, use_global_device_ids=true | all-gather | bytes 147456 | tf_op jit(solution)/shard_map/while/body/eval_jaxpr/all_gather | solution.py:55
  1135.3 24.9 %reduce-scatter.3.cloned.1.call-done = bf16[8,4096]{1,0:T(8,128)(2,1)} async-done(((bf16[64,4096]{1,0:T(8,128)(2,1)}), bf16[8,4096]{1,0:T(8,128)(2,1)}) %reduce-scatter.3.cloned.1.call-update) | async-done | bytes 65552 | tf_op jit(solution)/shard_map/while/body/eval_jaxpr/reduce_scatter | solution.py:126
  1162.2 18.6 %all_gather.51 = bf16[64,4096]{1,0:T(8,128)(2,1)S(1)} all-gather(bf16[8,4096]{1,0:T(8,128)(2,1)S(1)} %multiply_convert_fusion.2), channel_id=1, replica_groups=mesh['section'=4,'mp'=8] {'mp'}, dimensions={0}, use_global_device_ids=true | all-gather | bytes 589824 | tf_op jit(solution)/shard_map/while/body/eval_jaxpr/all_gather | solution.py:137
  1197.0 25.7 %reduce-scatter.5.cloned.1.call-done = bf16[8,4096]{1,0:T(8,128)(2,1)} async-done(((bf16[64,4096]{1,0:T(8,128)(2,1)}), bf16[8,4096]{1,0:T(8,128)(2,1)}) %reduce-scatter.5.cloned.1.call-update) | async-done | bytes 65552 | tf_op jit(solution)/shard_map/while/body/eval_jaxpr/reduce_scatter | solution.py:145
  1226.8 19.6 %all_gather.43 = bf16[1,64,4096]{2,1,0:T(8,128)(2,1)S(1)} all-gather(bf16[1,8,4096]{2,1,0:T(8,128)(2,1)S(1)} %get-tuple-element.431), channel_id=1, replica_groups=mesh['section'=4,'mp'=8] {'mp'}, dimensions={1}, use_global_device_ids=true | all-gather | bytes 589824 | tf_op jit(solution)/shard_map/all_gather | solution.py:183
  (451 shorter events, 324.7 us)
Async XLA Ops:
  34.2 79.1 %reduce-scatter.3.cloned.1.call-start = ((), (), s32[]{:S(2)}) async-start(), calls=%async_computation.2 | async-start | bytes 589824 | tf_op jit(solution)/shard_map/while/body/eval_jaxpr/reduce_scatter | solution.py:126
  86.7 89.1 %reduce-scatter.5.cloned.1.call-start = ((), (), s32[]{:S(2)}) async-start(), calls=%async_computation.3 | async-start | bytes 589824 | tf_op jit(solution)/shard_map/while/body/eval_jaxpr/reduce_scatter | solution.py:145
  115.3 30.7 %slice-start = ((s8[14680064]{0:T(1024)(128)(4,1)}), s8[4194304]{0:T(1024)(128)(4,1)S(1)}, s32[]{:S(2)}) async-start(s8[14680064]{0:T(1024)(128)(4,1)} %bitcast.79), calls=%async_computation.4 | async-start | bytes 8388608 | tf_op jit(solution)/shard_map/while
  146.0 29.8 %copy-start.2 = (bf16[8,4096]{1,0:T(8,128)(2,1)S(1)}, bf16[8,4096]{1,0:T(8,128)(2,1)}, u32[]{:S(2)}) copy-start(bf16[8,4096]{1,0:T(8,128)(2,1)} %reduce-scatter.3.cloned.1.call-done) | copy-start | bytes 196612 | tf_op jit(solution)/shard_map/while
  149.8 27.0 %collective-permute-start.1 = (bf16[1,8,4096]{2,1,0:T(8,128)(2,1)S(1)}, bf16[1,8,4096]{2,1,0:T(8,128)(2,1)S(1)}, u32[]{:S(2)}, u32[]{:S(2)}) collective-permute-start(bf16[1,8,4096]{2,1,0:T(8,128)(2,1)S(1)} %bitcast_select_fusion.4), channel_id=1, source_target_pairs={{0,24},{8,0},{16,8},{24,16},{1,25},{9,1},{17,9},{25,17},{2,26},{10... | collective-permute-start | bytes 196616 | tf_op jit(solution)/shard_map/while/body/eval_jaxpr/ppermute | solution.py:18
  176.7 3.2 collective-permute-start
  179.9 83.2 %reduce-scatter.3.cloned.1.call-start = ((), (), s32[]{:S(2)}) async-start(), calls=%async_computation.2 | async-start | bytes 589824 | tf_op jit(solution)/shard_map/while/body/eval_jaxpr/reduce_scatter | solution.py:126
  236.7 88.8 %reduce-scatter.5.cloned.1.call-start = ((), (), s32[]{:S(2)}) async-start(), calls=%async_computation.3 | async-start | bytes 589824 | tf_op jit(solution)/shard_map/while/body/eval_jaxpr/reduce_scatter | solution.py:145
  265.0 30.8 %slice-start = ((s8[14680064]{0:T(1024)(128)(4,1)}), s8[4194304]{0:T(1024)(128)(4,1)S(1)}, s32[]{:S(2)}) async-start(s8[14680064]{0:T(1024)(128)(4,1)} %bitcast.79), calls=%async_computation.4 | async-start | bytes 8388608 | tf_op jit(solution)/shard_map/while
  295.7 29.9 %copy-start.2 = (bf16[8,4096]{1,0:T(8,128)(2,1)S(1)}, bf16[8,4096]{1,0:T(8,128)(2,1)}, u32[]{:S(2)}) copy-start(bf16[8,4096]{1,0:T(8,128)(2,1)} %reduce-scatter.3.cloned.1.call-done) | copy-start | bytes 196612 | tf_op jit(solution)/shard_map/while
  299.5 27.1 %collective-permute-start.1 = (bf16[1,8,4096]{2,1,0:T(8,128)(2,1)S(1)}, bf16[1,8,4096]{2,1,0:T(8,128)(2,1)S(1)}, u32[]{:S(2)}, u32[]{:S(2)}) collective-permute-start(bf16[1,8,4096]{2,1,0:T(8,128)(2,1)S(1)} %bitcast_select_fusion.4), channel_id=1, source_target_pairs={{0,24},{8,0},{16,8},{24,16},{1,25},{9,1},{17,9},{25,17},{2,26},{10... | collective-permute-start | bytes 196616 | tf_op jit(solution)/shard_map/while/body/eval_jaxpr/ppermute | solution.py:18
  326.4 3.2 collective-permute-start
  329.6 83.0 %reduce-scatter.3.cloned.1.call-start = ((), (), s32[]{:S(2)}) async-start(), calls=%async_computation.2 | async-start | bytes 589824 | tf_op jit(solution)/shard_map/while/body/eval_jaxpr/reduce_scatter | solution.py:126
  386.1 89.2 %reduce-scatter.5.cloned.1.call-start = ((), (), s32[]{:S(2)}) async-start(), calls=%async_computation.3 | async-start | bytes 589824 | tf_op jit(solution)/shard_map/while/body/eval_jaxpr/reduce_scatter | solution.py:145
  414.6 30.8 %slice-start = ((s8[14680064]{0:T(1024)(128)(4,1)}), s8[4194304]{0:T(1024)(128)(4,1)S(1)}, s32[]{:S(2)}) async-start(s8[14680064]{0:T(1024)(128)(4,1)} %bitcast.79), calls=%async_computation.4 | async-start | bytes 8388608 | tf_op jit(solution)/shard_map/while
  445.4 29.9 %copy-start.2 = (bf16[8,4096]{1,0:T(8,128)(2,1)S(1)}, bf16[8,4096]{1,0:T(8,128)(2,1)}, u32[]{:S(2)}) copy-start(bf16[8,4096]{1,0:T(8,128)(2,1)} %reduce-scatter.3.cloned.1.call-done) | copy-start | bytes 196612 | tf_op jit(solution)/shard_map/while
  449.2 27.0 %collective-permute-start.1 = (bf16[1,8,4096]{2,1,0:T(8,128)(2,1)S(1)}, bf16[1,8,4096]{2,1,0:T(8,128)(2,1)S(1)}, u32[]{:S(2)}, u32[]{:S(2)}) collective-permute-start(bf16[1,8,4096]{2,1,0:T(8,128)(2,1)S(1)} %bitcast_select_fusion.4), channel_id=1, source_target_pairs={{0,24},{8,0},{16,8},{24,16},{1,25},{9,1},{17,9},{25,17},{2,26},{10... | collective-permute-start | bytes 196616 | tf_op jit(solution)/shard_map/while/body/eval_jaxpr/ppermute | solution.py:18
  476.1 3.2 collective-permute-start
  479.3 82.9 %reduce-scatter.3.cloned.1.call-start = ((), (), s32[]{:S(2)}) async-start(), calls=%async_computation.2 | async-start | bytes 589824 | tf_op jit(solution)/shard_map/while/body/eval_jaxpr/reduce_scatter | solution.py:126
  535.8 88.9 %reduce-scatter.5.cloned.1.call-start = ((), (), s32[]{:S(2)}) async-start(), calls=%async_computation.3 | async-start | bytes 589824 | tf_op jit(solution)/shard_map/while/body/eval_jaxpr/reduce_scatter | solution.py:145
  564.1 30.8 %slice-start = ((s8[14680064]{0:T(1024)(128)(4,1)}), s8[4194304]{0:T(1024)(128)(4,1)S(1)}, s32[]{:S(2)}) async-start(s8[14680064]{0:T(1024)(128)(4,1)} %bitcast.79), calls=%async_computation.4 | async-start | bytes 8388608 | tf_op jit(solution)/shard_map/while
  594.8 29.9 %copy-start.2 = (bf16[8,4096]{1,0:T(8,128)(2,1)S(1)}, bf16[8,4096]{1,0:T(8,128)(2,1)}, u32[]{:S(2)}) copy-start(bf16[8,4096]{1,0:T(8,128)(2,1)} %reduce-scatter.3.cloned.1.call-done) | copy-start | bytes 196612 | tf_op jit(solution)/shard_map/while
  598.6 27.0 %collective-permute-start.1 = (bf16[1,8,4096]{2,1,0:T(8,128)(2,1)S(1)}, bf16[1,8,4096]{2,1,0:T(8,128)(2,1)S(1)}, u32[]{:S(2)}, u32[]{:S(2)}) collective-permute-start(bf16[1,8,4096]{2,1,0:T(8,128)(2,1)S(1)} %bitcast_select_fusion.4), channel_id=1, source_target_pairs={{0,24},{8,0},{16,8},{24,16},{1,25},{9,1},{17,9},{25,17},{2,26},{10... | collective-permute-start | bytes 196616 | tf_op jit(solution)/shard_map/while/body/eval_jaxpr/ppermute | solution.py:18
  625.6 3.2 collective-permute-start
  628.7 82.9 %reduce-scatter.3.cloned.1.call-start = ((), (), s32[]{:S(2)}) async-start(), calls=%async_computation.2 | async-start | bytes 589824 | tf_op jit(solution)/shard_map/while/body/eval_jaxpr/reduce_scatter | solution.py:126
  685.3 88.9 %reduce-scatter.5.cloned.1.call-start = ((), (), s32[]{:S(2)}) async-start(), calls=%async_computation.3 | async-start | bytes 589824 | tf_op jit(solution)/shard_map/while/body/eval_jaxpr/reduce_scatter | solution.py:145
  713.5 30.8 %slice-start = ((s8[14680064]{0:T(1024)(128)(4,1)}), s8[4194304]{0:T(1024)(128)(4,1)S(1)}, s32[]{:S(2)}) async-start(s8[14680064]{0:T(1024)(128)(4,1)} %bitcast.79), calls=%async_computation.4 | async-start | bytes 8388608 | tf_op jit(solution)/shard_map/while
  744.3 29.9 %copy-start.2 = (bf16[8,4096]{1,0:T(8,128)(2,1)S(1)}, bf16[8,4096]{1,0:T(8,128)(2,1)}, u32[]{:S(2)}) copy-start(bf16[8,4096]{1,0:T(8,128)(2,1)} %reduce-scatter.3.cloned.1.call-done) | copy-start | bytes 196612 | tf_op jit(solution)/shard_map/while
  748.1 27.1 %collective-permute-start.1 = (bf16[1,8,4096]{2,1,0:T(8,128)(2,1)S(1)}, bf16[1,8,4096]{2,1,0:T(8,128)(2,1)S(1)}, u32[]{:S(2)}, u32[]{:S(2)}) collective-permute-start(bf16[1,8,4096]{2,1,0:T(8,128)(2,1)S(1)} %bitcast_select_fusion.4), channel_id=1, source_target_pairs={{0,24},{8,0},{16,8},{24,16},{1,25},{9,1},{17,9},{25,17},{2,26},{10... | collective-permute-start | bytes 196616 | tf_op jit(solution)/shard_map/while/body/eval_jaxpr/ppermute | solution.py:18
  775.0 3.2 collective-permute-start
  778.2 83.0 %reduce-scatter.3.cloned.1.call-start = ((), (), s32[]{:S(2)}) async-start(), calls=%async_computation.2 | async-start | bytes 589824 | tf_op jit(solution)/shard_map/while/body/eval_jaxpr/reduce_scatter | solution.py:126
  834.8 89.0 %reduce-scatter.5.cloned.1.call-start = ((), (), s32[]{:S(2)}) async-start(), calls=%async_computation.3 | async-start | bytes 589824 | tf_op jit(solution)/shard_map/while/body/eval_jaxpr/reduce_scatter | solution.py:145
  863.1 30.8 %slice-start = ((s8[14680064]{0:T(1024)(128)(4,1)}), s8[4194304]{0:T(1024)(128)(4,1)S(1)}, s32[]{:S(2)}) async-start(s8[14680064]{0:T(1024)(128)(4,1)} %bitcast.79), calls=%async_computation.4 | async-start | bytes 8388608 | tf_op jit(solution)/shard_map/while
  893.9 29.9 %copy-start.2 = (bf16[8,4096]{1,0:T(8,128)(2,1)S(1)}, bf16[8,4096]{1,0:T(8,128)(2,1)}, u32[]{:S(2)}) copy-start(bf16[8,4096]{1,0:T(8,128)(2,1)} %reduce-scatter.3.cloned.1.call-done) | copy-start | bytes 196612 | tf_op jit(solution)/shard_map/while
  897.7 27.0 %collective-permute-start.1 = (bf16[1,8,4096]{2,1,0:T(8,128)(2,1)S(1)}, bf16[1,8,4096]{2,1,0:T(8,128)(2,1)S(1)}, u32[]{:S(2)}, u32[]{:S(2)}) collective-permute-start(bf16[1,8,4096]{2,1,0:T(8,128)(2,1)S(1)} %bitcast_select_fusion.4), channel_id=1, source_target_pairs={{0,24},{8,0},{16,8},{24,16},{1,25},{9,1},{17,9},{25,17},{2,26},{10... | collective-permute-start | bytes 196616 | tf_op jit(solution)/shard_map/while/body/eval_jaxpr/ppermute | solution.py:18
  924.6 3.2 collective-permute-start
  927.8 83.0 %reduce-scatter.3.cloned.1.call-start = ((), (), s32[]{:S(2)}) async-start(), calls=%async_computation.2 | async-start | bytes 589824 | tf_op jit(solution)/shard_map/while/body/eval_jaxpr/reduce_scatter | solution.py:126
  984.3 88.9 %reduce-scatter.5.cloned.1.call-start = ((), (), s32[]{:S(2)}) async-start(), calls=%async_computation.3 | async-start | bytes 589824 | tf_op jit(solution)/shard_map/while/body/eval_jaxpr/reduce_scatter | solution.py:145
  1012.7 30.8 %slice-start = ((s8[14680064]{0:T(1024)(128)(4,1)}), s8[4194304]{0:T(1024)(128)(4,1)S(1)}, s32[]{:S(2)}) async-start(s8[14680064]{0:T(1024)(128)(4,1)} %bitcast.79), calls=%async_computation.4 | async-start | bytes 8388608 | tf_op jit(solution)/shard_map/while
  1043.4 29.8 %copy-start.2 = (bf16[8,4096]{1,0:T(8,128)(2,1)S(1)}, bf16[8,4096]{1,0:T(8,128)(2,1)}, u32[]{:S(2)}) copy-start(bf16[8,4096]{1,0:T(8,128)(2,1)} %reduce-scatter.3.cloned.1.call-done) | copy-start | bytes 196612 | tf_op jit(solution)/shard_map/while
  1047.2 27.1 %collective-permute-start.1 = (bf16[1,8,4096]{2,1,0:T(8,128)(2,1)S(1)}, bf16[1,8,4096]{2,1,0:T(8,128)(2,1)S(1)}, u32[]{:S(2)}, u32[]{:S(2)}) collective-permute-start(bf16[1,8,4096]{2,1,0:T(8,128)(2,1)S(1)} %bitcast_select_fusion.4), channel_id=1, source_target_pairs={{0,24},{8,0},{16,8},{24,16},{1,25},{9,1},{17,9},{25,17},{2,26},{10... | collective-permute-start | bytes 196616 | tf_op jit(solution)/shard_map/while/body/eval_jaxpr/ppermute | solution.py:18
  1074.1 3.2 collective-permute-start
  1077.3 82.9 %reduce-scatter.3.cloned.1.call-start = ((), (), s32[]{:S(2)}) async-start(), calls=%async_computation.2 | async-start | bytes 589824 | tf_op jit(solution)/shard_map/while/body/eval_jaxpr/reduce_scatter | solution.py:126
  1133.9 88.8 %reduce-scatter.5.cloned.1.call-start = ((), (), s32[]{:S(2)}) async-start(), calls=%async_computation.3 | async-start | bytes 589824 | tf_op jit(solution)/shard_map/while/body/eval_jaxpr/reduce_scatter | solution.py:145
  1162.1 30.8 %slice-start = ((s8[14680064]{0:T(1024)(128)(4,1)}), s8[4194304]{0:T(1024)(128)(4,1)S(1)}, s32[]{:S(2)}) async-start(s8[14680064]{0:T(1024)(128)(4,1)} %bitcast.79), calls=%async_computation.4 | async-start | bytes 8388608 | tf_op jit(solution)/shard_map/while
  1192.9 29.9 %copy-start.2 = (bf16[8,4096]{1,0:T(8,128)(2,1)S(1)}, bf16[8,4096]{1,0:T(8,128)(2,1)}, u32[]{:S(2)}) copy-start(bf16[8,4096]{1,0:T(8,128)(2,1)} %reduce-scatter.3.cloned.1.call-done) | copy-start | bytes 196612 | tf_op jit(solution)/shard_map/while
  1196.7 27.0 %collective-permute-start.1 = (bf16[1,8,4096]{2,1,0:T(8,128)(2,1)S(1)}, bf16[1,8,4096]{2,1,0:T(8,128)(2,1)S(1)}, u32[]{:S(2)}, u32[]{:S(2)}) collective-permute-start(bf16[1,8,4096]{2,1,0:T(8,128)(2,1)S(1)} %bitcast_select_fusion.4), channel_id=1, source_target_pairs={{0,24},{8,0},{16,8},{24,16},{1,25},{9,1},{17,9},{25,17},{2,26},{10... | collective-permute-start | bytes 196616 | tf_op jit(solution)/shard_map/while/body/eval_jaxpr/ppermute | solution.py:18
  1223.6 3.2 collective-permute-start
  (30 other events, 396.3 us)
Sparse Core Ops, SparseCore 0:
  86.8 26.4 reduce-scatter.2
  149.9 25.9 reduce-scatter.4
  236.8 26.1 reduce-scatter.2
  299.6 25.9 reduce-scatter.4
  386.2 26.4 reduce-scatter.2
  449.2 25.9 reduce-scatter.4
  535.9 26.1 reduce-scatter.2
  598.7 25.9 reduce-scatter.4
  685.4 26.1 reduce-scatter.2
  748.2 25.9 reduce-scatter.4
  834.9 26.2 reduce-scatter.2
  897.8 25.9 reduce-scatter.4
  984.4 26.2 reduce-scatter.2
  1047.3 25.8 reduce-scatter.4
  1134.0 26.1 reduce-scatter.2
  1196.8 25.9 reduce-scatter.4
where the time goes:
time: 1260 us; the launch traced here: 1250 us
  blocking collectives  527 us (42%)
  waiting for transfers between devices  430 us (34%)
  matrix products  192 us (15%)
  other arithmetic  70.8 us (6%)
  local copies, waits for them, and re-layouts  15.3 us (1%)
  between operations  13.1 us (1%)
    reduce_scatter x8, waiting for transfers between devices, layer_rows(): lax.psum_scatter(jnp.dot(hidden, w_down[layer_pos], preferred_element_typ...  206 us
    reduce_scatter x8, waiting for transfers between devices, layer_rows(): lax.psum_scatter(jnp.dot(context, w_out[layer_pos], preferred_element_typ...  200 us
    all_gather x8, blocking collectives, layer_rows(): lax.all_gather(normed, 'mp', axis=0, tiled=True)  153 us
    all_gather x8, blocking collectives, layer_rows(): lax.all_gather(normed_ffn, 'mp', axis=0, tiled=True)  149 us
    all_gather x8, blocking collectives, attend_local(): lax.all_gather(key_local, 'mp', axis=1, tiled=True)  103 us
    all_gather x8, blocking collectives, attend_local(): lax.all_gather(value_local, 'mp', axis=1, tiled=True)  103 us
    dot_general x8, matrix products, layer_rows(): jnp.dot(lax.all_gather(normed_ffn, 'mp', axis=0, tiled=True), joined_pair...  97.2 us
    dot_general x8, matrix products, layer_rows(): jnp.dot(lax.all_gather(normed, 'mp', axis=0, tiled=True), joined_qkv[laye...  31.8 us
  transfers between devices with their start and end apart: 32, of which 24 were waited for; matrix products, arithmetic and copies ran while one was open for 1% of the time, Pallas kernels for 0%

commit v1 on v0

--- a/solution.py
+++ b/solution.py
@@ -1,6 +1,9 @@
 import jax
 import jax.numpy as jnp
+import numpy as np
 from jax import lax
+from jax.experimental import pallas as pl
+from jax.experimental.pallas import tpu as pltpu
 from jax.sharding import PartitionSpec as P
 
 HEADS = 32
@@ -184,9 +187,445 @@
     return result.reshape(hidden_in.shape)
 
 
+MESH = pl.DeviceIdType.MESH
+BF16 = jnp.bfloat16
+F32 = jnp.float32
+TILE = 256
+WIDE = 512
+
+
+def tables(length):
+    half = HD // 2
+    frequency = np.float32(ROPE_BASE) ** (-(np.arange(half, dtype=np.float32) / np.float32(half)))
+    angles = np.arange(length, dtype=np.float32)[:, None] * frequency[None, :].astype(np.float32)
+    cosine, sine = np.cos(angles), np.sin(angles)
+    q_cos = np.concatenate([cosine, cosine], axis=1)
+    q_sin = np.concatenate([-sine, sine], axis=1)
+    k_cos = np.concatenate([q_cos.T, np.ones((HD, length))], axis=1)
+    k_sin = np.concatenate([q_sin.T, np.zeros((HD, length))], axis=1)
+    return [jnp.asarray(t, F32) for t in (q_cos, q_sin, k_cos, k_sin)]
+
+
+def remote(src, dst, send_sem, recv_sem, where):
+    return pltpu.make_async_remote_copy(
+        src_ref=src,
+        dst_ref=dst,
+        send_sem=send_sem,
+        recv_sem=recv_sem,
+        device_id=where,
+        device_id_type=MESH,
+    )
+
+
+def layer_kernel(
+    sections,
+    peers,
+    heads_on,
+    ffn_blocks,
+    hidden_in,
+    attn_gain,
+    ffn_gain,
+    q_cos,
+    q_sin,
+    k_cos,
+    k_sin,
+    w_query,
+    w_key,
+    w_value,
+    w_out,
+    w_gate,
+    w_up,
+    w_down,
+    out,
+    v_query,
+    v_kv,
+    v_out,
+    v_gate,
+    v_up,
+    v_down,
+    inbox,
+    outbox,
+    home,
+    rows_f32,
+    gathered,
+    normed,
+    kv_send,
+    kv_recv,
+    context,
+    hidden,
+    part,
+    pair_in,
+    chip_send,
+    chip_in,
+    weight_sem,
+    inbox_sem,
+    outbox_sem,
+    seed_sem,
+    home_sem,
+    gather_send,
+    gather_recv,
+    relay_send,
+    relay_recv,
+    kv_send_sem,
+    kv_recv_sem,
+    pair_sem,
+    chip_send_sem,
+    chip_recv_sem,
+    out_sem,
+):
+    sec = lax.axis_index("section")
+    me = lax.axis_index("mp")
+    chips = peers // 2
+    chip, core = me // 2, me % 2
+    slot = core * chips + chip
+    mate = (sec, chip * 2 + 1 - core)
+    last = sections - 1
+    rows, width = rows_f32.shape
+    length = peers * rows
+    heads_here = v_query.shape[1] // HD
+    key_width = w_key.shape[1]
+    units = v_gate.shape[1]
+
+    def chip_at(step):
+        other = (chip + step) % chips
+        return other, (sec, other * 2 + core)
+
+    def weight_copies():
+        pairs = (
+            (w_query, v_query),
+            (w_key, v_kv.at[:, pl.ds(0, key_width)]),
+            (w_value, v_kv.at[:, pl.ds(key_width, key_width)]),
+            (w_out, v_out),
+            (w_gate, v_gate),
+            (w_up, v_up),
+            (w_down, v_down),
+        )
+        return [
+            pltpu.make_async_copy(a, b, weight_sem.at[i]) for i, (a, b) in enumerate(pairs)
+        ]
+
+    seed = pltpu.make_async_copy(hidden_in.at[slot], home, seed_sem)
+    seed.start()
+    for copy in weight_copies():
+        copy.start()
+
+    barrier = pltpu.get_barrier_semaphore()
+    for step in range(1, peers):
+        pl.semaphore_signal(barrier, inc=1, device_id=(sec, (me + step) % peers), device_id_type=MESH)
+    for step in range(1, sections):
+        pl.semaphore_signal(barrier, inc=1, device_id=((sec + step) % sections, me), device_id_type=MESH)
+    pl.semaphore_wait(barrier, peers + sections - 2)
+
+    seed.wait()
+    own = remote(home, inbox.at[sec], outbox_sem.at[0], inbox_sem.at[sec], (0, me))
+
+    @pl.when(sec == 0)
+    def _():
+        inbox[0] = home[...]
+
+    @pl.when(sec != 0)
+    def _():
+        own.start()
+        own.wait_send()
+
+    def all_gather():
+        mine = gathered.at[slot]
+        to_mate = remote(mine, mine, gather_send.at[chips - 1], gather_recv.at[chips - 1], mate)
+        sends = []
+        for k in (list(range(1, chips, 2)) + list(range(2, chips, 2))):
+            _, where = chip_at(k)
+            sends.append(remote(mine, mine, gather_send.at[k - 1], gather_recv.at[k - 1], where))
+            sends[-1].start()
+        to_mate.start()
+        relays = []
+        for k in (list(range(1, chips, 2)) + list(range(2, chips, 2))):
+            other, where = chip_at(chips - k)
+            block = gathered.at[core * chips + other]
+            remote(block, block, gather_send.at[k - 1], gather_recv.at[k - 1], where).wait_recv()
+            relays.append(remote(block, block, relay_send.at[k - 1], relay_recv.at[k - 1], mate))
+            relays[-1].start()
+        to_mate.wait_recv()
+        for k in range(1, chips):
+            other, _ = chip_at(chips - k)
+            block = gathered.at[(1 - core) * chips + other]
+            remote(block, block, relay_send.at[k - 1], relay_recv.at[k - 1], mate).wait_recv()
+        for copy in sends + relays + [to_mate]:
+            copy.wait_send()
+
+    def widen():
+        columns = width // 4
+        for i in range(4):
+            at = pl.ds(i * columns, columns)
+            block = gathered[:, :, at].astype(F32)
+            normed[:, at] = block.reshape(length, columns).astype(BF16)
+
+    def norm_rows(gain):
+        x = rows_f32[...]
+        scale = lax.rsqrt(jnp.mean(x * x, axis=-1, keepdims=True) + EPSILON)
+        gathered[slot] = (x * scale * gain[...].astype(F32)).astype(BF16)
+
+    def reduce_rows():
+        other_half = part.at[pl.ds((1 - core) * chips, chips)]
+        across = remote(other_half, pair_in, pair_sem.at[0], pair_sem.at[1], mate)
+        across.start()
+        across.wait_recv()
+        for k in range(1, chips):
+            other, where = chip_at(k)
+            both = part[core * chips + other].astype(F32) + pair_in[other].astype(F32)
+            chip_send[k - 1] = both.astype(BF16)
+            remote(
+                chip_send.at[k - 1], chip_in.at[k - 1], chip_send_sem.at[k - 1], chip_recv_sem.at[k - 1], where
+            ).start()
+        rows_f32[...] = rows_f32[...] + (part[slot].astype(F32) + pair_in[chip].astype(F32))
+        for k in range(1, chips):
+            _, where = chip_at(k)
+            remote(
+                chip_send.at[k - 1], chip_in.at[k - 1], chip_send_sem.at[k - 1], chip_recv_sem.at[k - 1], where
+            ).wait()
+            rows_f32[...] = rows_f32[...] + chip_in[k - 1].astype(F32)
+        across.wait_send()
+
+    def project_rows(left, weight):
+        def step(i, _):
+            at = pl.ds(pl.multiple_of(i * WIDE, WIDE), WIDE)
+            term = jnp.dot(left[...], weight[:, at], preferred_element_type=F32)
+            part[:, :, at] = term.reshape(peers, rows, WIDE).astype(BF16)
+            return 0
+
+        lax.fori_loop(0, width // WIDE, step, 0)
+
+    def exchange_kv():
+        copies = []
+        for step in range(1, peers):
+            to = (me + step) % peers
+            copies.append(
+                remote(
+                    kv_send.at[to], kv_recv.at[me], kv_send_sem.at[step - 1], kv_recv_sem.at[step - 1], (sec, to)
+                )
+            )
+            copies[-1].start()
+        kv_recv[me] = kv_send[me]
+        return copies
+
+    def attention(active):
+        left = normed[...]
+        kv = jnp.dot(left, v_kv[...], preferred_element_type=F32).astype(BF16)
+        stacked = jnp.concatenate([kv[:, :key_width], kv[:, key_width:]], axis=0)
+        r = lax.broadcasted_iota(jnp.int32, (key_width, key_width), 0)
+        c = lax.broadcasted_iota(jnp.int32, (key_width, key_width), 1)
+        parts_here = key_width // KV_HEADS
+        pick = jnp.where(c == (r % parts_here) * KV_HEADS + r // parts_here, 1.0, 0.0).astype(BF16)
+        by_head = lax.dot_general(
+            pick, stacked, (((1,), (1,)), ((), ())), preferred_element_type=F32
+        )
+        kv_send[...] = by_head.astype(BF16).reshape(KV_HEADS, parts_here, 2 * length)
+        copies = exchange_kv()
+        query = jnp.dot(left, v_query[...], preferred_element_type=F32)
+        heads = []
+        for h in range(heads_here):
+            head = query[:, h * HD : (h + 1) * HD]
+            heads.append(
+                (head * q_cos[...] + pltpu.roll(head, HD // 2, 1) * q_sin[...]).astype(BF16)
+            )
+        queries = jnp.concatenate(heads, axis=0)
+        for copy in copies:
+            copy.wait()
+        pair = kv_recv[...].reshape(HD, 2 * length).astype(F32)
+        swapped = jnp.concatenate([pair[HD // 2 :], pair[: HD // 2]], axis=0)
+        pair = (pair * k_cos[...] + swapped * k_sin[...]).astype(BF16)
+        scores = jnp.dot(queries, pair, preferred_element_type=F32) * HD ** (-0.5)
+        token = lax.broadcasted_iota(jnp.int32, scores.shape, 0) % length
+        key_at = lax.broadcasted_iota(jnp.int32, scores.shape, 1)
+        scores = jnp.where(key_at <= token, scores, -jnp.inf)
+        scores = jnp.exp(scores - jnp.max(scores, axis=-1, keepdims=True))
+        chances = scores / jnp.sum(scores, axis=-1, keepdims=True)
+        chances = pltpu.roll(chances, length, 1).astype(BF16)
+        mixed = lax.dot_general(
+            chances, pair, (((1,), (1,)), ((), ())), preferred_element_type=F32
+        )
+        for h in range(heads_here):
+            on = me * heads_here + h < active
+            block = mixed[h * length : (h + 1) * length]
+            context[:, h * HD : (h + 1) * HD] = jnp.where(on, block, 0.0).astype(BF16)
+
+    def feed_forward(block_count):
+        def step(i, _):
+            at = pl.ds(pl.multiple_of(i * TILE, TILE), TILE)
+            left = normed[...]
+            gate = jnp.dot(left, v_gate[:, at], preferred_element_type=F32)
+            up = jnp.dot(left, v_up[:, at], preferred_element_type=F32)
+            unit = me * units + i * TILE + lax.broadcasted_iota(jnp.int32, gate.shape, 1)
+            value = gate / (1.0 + jnp.exp(-gate)) * up
+            hidden[:, at] = jnp.where(unit < BLOCK * block_count, value, 0.0).astype(BF16)
+            return 0
+
+        lax.fori_loop(0, units // TILE, step, 0)
+
+    def micro_step(m, _):
+        arrived = remote(home, inbox.at[m], outbox_sem.at[0], inbox_sem.at[m], (0, me))
+
+        @pl.when((sec != 0) | (m != 0))
+        def _():
+            arrived.wait_recv()
+
+        rows_f32[...] = inbox[m].astype(F32)
+        norm_rows(attn_gain)
+        all_gather()
+        widen()
+
+        def when_loaded(first, stop):
+            @pl.when(m == 0)
+            def _():
+                for copy in weight_copies()[first:stop]:
+                    copy.wait()
+
+        when_loaded(0, 3)
+        attention(heads_on[m, 0])
+        when_loaded(3, 4)
+        project_rows(context, v_out)
+        reduce_rows()
+        norm_rows(ffn_gain)
+        all_gather()
+        widen()
+        when_loaded(4, 6)
+        feed_forward(ffn_blocks[m, 0])
+        when_loaded(6, 7)
+        project_rows(hidden, v_down)
+        reduce_rows()
+        outbox[m] = rows_f32[...].astype(BF16)
+
+        @pl.when(sec < last)
+        def _():
+            remote(outbox.at[m], inbox.at[m], outbox_sem.at[m], inbox_sem.at[m], (sec + 1, me)).start()
+
+        @pl.when((sec == last) & (m < last))
+        def _():
+            remote(outbox.at[m], home, outbox_sem.at[m], home_sem, (m, me)).start()
+
+        return 0
+
+    lax.fori_loop(0, sections, micro_step, 0)
+
+    for m in range(sections):
+        sent = remote(outbox.at[m], home, outbox_sem.at[m], home_sem, (0, me))
+        if m < last:
+            sent.wait_send()
+        else:
+
+            @pl.when(sec < last)
+            def _():
+                sent.wait_send()
+
+    @pl.when(sec < last)
+    def _():
+        remote(outbox.at[0], home, outbox_sem.at[0], home_sem, (last, me)).wait_recv()
+        gathered[slot] = home[...]
+
+    @pl.when(sec == last)
+    def _():
+        gathered[slot] = outbox[last]
+
+    all_gather()
+    done = pltpu.make_async_copy(gathered, out, out_sem)
+    done.start()
+    done.wait()
+
+
+def resident(hidden_in, attn_gain, w_query, w_key, w_value, w_out, ffn_gain, w_gate, w_up, w_down, ffn_blocks, heads_on):
+    sections, peers = lax.axis_size("section"), lax.axis_size("mp")
+    length, width = hidden_in.shape[2:]
+    rows, chips = length // peers, peers // 2
+    units, key_width = w_gate.shape[2], w_key.shape[2]
+    query_width = w_query.shape[2]
+    parts_here = key_width // KV_HEADS
+    smem = pl.BlockSpec(memory_space=pltpu.SMEM)
+    vmem = pl.BlockSpec(memory_space=pltpu.VMEM)
+    hbm = pl.BlockSpec(memory_space=pl.ANY)
+    dma = pltpu.SemaphoreType.DMA
+    half = pltpu.VMEM
+    result = pl.pallas_call(
+        lambda *refs: layer_kernel(sections, peers, *refs),
+        out_shape=jax.ShapeDtypeStruct((peers, rows, width), BF16),
+        in_specs=[smem, smem, hbm] + [vmem] * 6 + [hbm] * 7,
+        out_specs=hbm,
+        scratch_shapes=[
+            half((width, query_width), BF16),
+            half((width, 2 * key_width), BF16),
+            half((query_width, width), BF16),
+            half((width, units), BF16),
+            half((width, units), BF16),
+            half((units, width), BF16),
+            half((sections, rows, width), BF16),
+            half((sections, rows, width), BF16),
+            half((rows, width), BF16),
+            half((rows, width), F32),
+            half((peers, rows, width), BF16),
+            half((length, width), BF16),
+            half((peers, parts_here, 2 * length), BF16),
+            half((peers, parts_here, 2 * length), BF16),
+            half((length, query_width), BF16),
+            half((length, units), BF16),
+            half((peers, rows, width), BF16),
+            half((chips, rows, width), BF16),
+            half((chips - 1, rows, width), BF16),
+            half((chips - 1, rows, width), BF16),
+            dma((7,)),
+            dma((sections,)),
+            dma((sections,)),
+            dma,
+            dma,
+            dma((chips,)),
+            dma((chips,)),
+            dma((chips - 1,)),
+            dma((chips - 1,)),
+            dma((peers - 1,)),
+            dma((peers - 1,)),
+            dma((2,)),
+            dma((chips - 1,)),
+            dma((chips - 1,)),
+            dma,
+        ],
+        compiler_params=pltpu.CompilerParams(
+            collective_id=0, has_side_effects=True, vmem_limit_bytes=67043328
+        ),
+    )(
+        heads_on,
+        ffn_blocks,
+        hidden_in.reshape(peers, rows, width),
+        attn_gain,
+        ffn_gain,
+        *tables(length),
+        w_query[0],
+        w_key[0],
+        w_value[0],
+        w_out[0],
+        w_gate[0],
+        w_up[0],
+        w_down[0],
+    )
+    return result.reshape(hidden_in.shape)
+
+
+def one_device(*args):
+    hidden_in, w_query, w_key, w_gate = args[0], args[2], args[3], args[7]
+    sections, peers = lax.axis_size("section"), lax.axis_size("mp")
+    fits = (
+        hidden_in.shape[0] == 1
+        and args[10].shape[0] == sections
+        and peers == KV_HEADS
+        and hidden_in.shape[2] == 8 * peers
+        and 2 * hidden_in.shape[2] == HD
+        and w_query.shape[2] * KV_HEADS == HEADS * HD
+        and w_key.shape[2] == HD
+        and w_gate.shape[2] % TILE == 0
+        and hidden_in.shape[3] % WIDE == 0
+    )
+    return (resident if fits else per_device)(*args)
+
+
 def solution(mesh):
     return jax.shard_map(
-        per_device,
+        one_device,
         mesh=mesh,
         in_specs=(
             P(None, "section", None, None),

time: 1260 us -> 391 us (0.31)
  blocking collectives: 527 us -> 0 us
  waiting for transfers between devices: 430 us -> 0 us
  Pallas kernels: 0 us -> 386 us
  matrix products: 192 us -> 0 us
  other arithmetic: 70.8 us -> 0 us
  between operations: 13.1 us -> 0.01 us
    all_gather x33 -> x0, blocking collectives: 527 us -> none  [the longest x8 153 us: layer_rows(): lax.all_gather(normed, 'mp', axis=0, tiled=True)]
    reduce_scatter x16 -> x0, waiting for transfers between devices: 406 us -> none  [the longest x8 206 us: layer_rows(): lax.psum_scatter(jnp.dot(hidden, w_down[layer_pos], preferred_element_typ...]
    pallas_call x0 -> x1, Pallas kernels: none -> 386 us  [resident(): pl.pallas_call(lambda *refs: layer_kernel(sections, peers, *refs), out_sh...]
    dot_general x40 -> x0, matrix products: 189 us -> none  [the longest x8 97.2 us: layer_rows(): jnp.dot(lax.all_gather(normed_ffn, 'mp', axis=0, tiled=True), joined_pair...]
    concatenate x18 -> x0, other arithmetic: 28.5 us -> none  [the longest x1 20.1 us: per_device(): joined_pair = [jnp.concatenate([w_gate[0], w_up[0]], axis=1)]]
    ppermute x16 -> x0, waiting for transfers between devices: 24.5 us -> none  [passed_along(): lax.ppermute(array, axis, [(i, (i + by) % peers) for i in range(peers)])]
    convert_element_type x40 -> x0, other arithmetic: 15.3 us -> none  [the longest x8 7.41 us: layer_rows(): normed_ffn = rms_scale(attended, ffn_gain[layer_pos]).astype(jnp.bfloat16)]
  transfers between devices with their start and end apart: 32 -> 0, of which waited for: 24 -> 0; matrix products, arithmetic and copies ran while one was open for 1% -> 0% of each run, Pallas kernels for 0% -> 0%
where the time goes in v1:
time: 391 us
  Pallas kernels  386 us (99%)
  local copies, waits for them, and re-layouts  4.51 us (1%)
    pallas_call x1, Pallas kernels, resident(): pl.pallas_call(lambda *refs: layer_kernel(sections, peers, *refs), out_sh...  386 us

profile of v1, /device:TPU:7, one launch (start us, length us, event | category | flops | bytes accessed | tf_op | source)
XLA Modules:
  0.0 390.5 jit_solution(10078659912484152702)
XLA Ops:
  0.0 1.3 copy.18.refs_1_
  1.3 1.3 copy.17.refs_0_
  2.6 386.0 %shard_map.154 = bf16[8,8,4096]{2,1,0:T(8,128)(2,1)} custom-call(s32[4,1]{1,0:T(4,128)} %copy.17.refs_0_, s32[4,1]{1,0:T(4,128)} %copy.18.refs_1_, bf16[8,8,4096]{2,1,0:T(8,128)(2,1)} %bitcast.17, bf16[1,4096]{1,0:T(2,128)(2,1)} %refs_3_.1, bf16[1,4096]{1,0:T(2,128)(2,1)} %refs_4_.1, f32[64,128]{1,0:T(8,128)} %constant.8.clone.refs_5_, ...), custom_call_target="tpu_custom_call" | custom-call | tf_op jit(solution)/shard_map/pallas_call | solution.py:546
  388.7 1.9 copy.20
